TPU v7x, 32 devices: a whole 2x2x4 slice. The times are simulated.
32 devices in a mesh: dp: 4 (over z), expert: 8 (over y, x, core).
Axes of the slice: x: 2, y: 2, z: 4, core: 2. Of those that a mesh axis runs over, the one named last changes fastest.
Arguments:
- grad_output: bfloat16 [8, 8, 3840], P('expert', None, 'dp'), may hold values from -6 to 6
- router_logits: float32 [8, 8, 32], P('expert'), may hold values from -8 to 8
- expert_ids: int32 [8, 8, 8], P('expert'), may hold values from 0 to 31, all different within a row; in each aligned block of 8 rows (0 to 7, 8 to 15, ..., all dimensions but the last counted through in order) at most 3 rows name the same one
- router_input: bfloat16 [8, 8, 3840], P('expert', 'dp'), may hold values from -6 to 6
- router_weight: bfloat16 [32, 3840], P(None, 'dp'), may hold values from -0.09375 to 0.09375
- gate_weight: bfloat16 [32, 3840, 1024], P('expert', 'dp'), may hold values from -0.09375 to 0.09375
- up_weight: bfloat16 [32, 3840, 1024], P('expert', 'dp'), may hold values from -0.09375 to 0.09375
- down_weight: bfloat16 [32, 1024, 3840], P('expert', None, 'dp'), may hold values from -0.1875 to 0.1875
- gate_saved: bfloat16 [32, 24, 1024], P('expert'), may hold values from -6 to 6
- up_saved: bfloat16 [32, 24, 1024], P('expert'), may hold values from -6 to 6
Outputs:
- grad_input: bfloat16 [8, 8, 3840], P('expert', None, 'dp')
- grad_router: float32 [32, 3840], P('expert', 'dp')
Inputs may be any that keep to these rules, and one draw needn't show every extreme that they name: `expert_ids`: within one token group (the 8 tokens of one index of expert, in order), no expert is named more than 3 times, a bound that some block reaches; every row names 8 different experts.
All inputs are finite; a program needn't handle non-finite values.
Results may differ from a plain program's by a relative error of at most 0.008.
Values may be sent and summed in bfloat16 or wider, within the bound.
No kernel may reach another device: no remote copies, remote signals or barrier semaphores. Data moves between devices by JAX's collectives and lax.ppermute only.
A program may use at most 64 MiB of HBM per device.

v0:
```python
import jax
import jax.numpy as jnp
from jax import lax
from jax.sharding import PartitionSpec as P

route_scale = 2.5


def split_pair(values):
    upper = values.astype(jnp.bfloat16)
    lower = (values - upper.astype(jnp.float32)).astype(jnp.bfloat16)
    return jnp.stack([upper, lower], axis=-1)


def join_pair(paired):
    return paired[..., 0].astype(jnp.float32) + paired[..., 1].astype(jnp.float32)


def activation_backward(hidden_grad, saved_gate, saved_up):
    gate_value = saved_gate.astype(jnp.float32)
    up_value = saved_up.astype(jnp.float32)
    gate_sigmoid = jax.nn.sigmoid(gate_value)
    activated = gate_value * gate_sigmoid
    hidden = lax.optimization_barrier((activated * up_value).astype(jnp.bfloat16)).astype(
        jnp.float32
    )
    gate_share = jnp.sum(hidden * hidden_grad, axis=1)
    gate_part = (
        hidden_grad * up_value * gate_sigmoid * (1.0 + gate_value * (1.0 - gate_sigmoid))
    ).astype(jnp.bfloat16)
    up_part = (hidden_grad * activated).astype(jnp.bfloat16)
    return (gate_part, up_part, gate_share)


def local(
    grad_output,
    router_logits,
    expert_ids,
    router_input,
    router_weight,
    gate_weight,
    up_weight,
    down_weight,
    gate_saved,
    up_saved,
):
    expert_count = lax.axis_size("expert")
    out_rows = grad_output[0]
    group_size, feature_share = out_rows.shape
    expert_total = router_logits.shape[2]
    top_count = expert_ids.shape[2]
    local_experts, slot_count, hidden_size = gate_saved.shape
    slot_depth = slot_count // expert_count
    assign_count = group_size * top_count
    flat_ids = expert_ids[0].reshape(assign_count)
    expert_hot = (flat_ids[:, None] == jnp.arange(expert_total, dtype=jnp.int32)[None, :]).astype(
        jnp.int32
    )
    earlier = jnp.cumsum(expert_hot, axis=0) - expert_hot
    ranking = jnp.sum(expert_hot * earlier, axis=1)
    target = flat_ids * slot_depth + ranking
    slot_place = (
        jnp.arange(expert_total * slot_depth, dtype=jnp.int32)[:, None] == target[None, :]
    ).astype(jnp.bfloat16)
    owner_hot = (
        (jnp.arange(assign_count, dtype=jnp.int32) // top_count)[:, None]
        == jnp.arange(group_size, dtype=jnp.int32)[None, :]
    ).astype(jnp.bfloat16)
    slot_token = jnp.dot(slot_place, owner_hot, preferred_element_type=jnp.float32).astype(
        jnp.bfloat16
    )
    outgoing = jnp.dot(slot_token, out_rows, preferred_element_type=jnp.float32).astype(
        jnp.bfloat16
    )
    incoming = lax.all_to_all(
        outgoing.reshape(expert_total, slot_depth, feature_share),
        "expert",
        split_axis=0,
        concat_axis=1,
        tiled=True,
    )
    partial_hidden = jnp.einsum(
        "esd,efd->esf", incoming, down_weight, preferred_element_type=jnp.float32
    )
    row_total = local_experts * slot_count
    hidden_grad = lax.psum(partial_hidden.reshape(row_total, hidden_size), "dp")
    grad_gate, grad_up, gate_grad = activation_backward(
        hidden_grad,
        gate_saved.reshape(row_total, hidden_size),
        up_saved.reshape(row_total, hidden_size),
    )
    grad_gate = grad_gate.reshape(local_experts, slot_count, hidden_size)
    grad_up = grad_up.reshape(local_experts, slot_count, hidden_size)
    gate_grad = gate_grad.reshape(local_experts, slot_count)
    expert_input = jnp.einsum(
        "esf,edf->esd", grad_gate, gate_weight, preferred_element_type=jnp.float32
    )
    expert_input = expert_input + jnp.einsum(
        "esf,edf->esd", grad_up, up_weight, preferred_element_type=jnp.float32
    )
    expert_input = expert_input.astype(jnp.bfloat16)
    rows_back, gate_paired_back = (
        lax.all_to_all(expert_input, "expert", split_axis=1, concat_axis=0, tiled=True),
        lax.all_to_all(split_pair(gate_grad), "expert", split_axis=1, concat_axis=0, tiled=True),
    )
    gate_back = join_pair(gate_paired_back)
    pick_map = slot_place.T.astype(jnp.float32)
    picked_gate = jnp.dot(
        pick_map, gate_back.reshape(expert_total * slot_depth), precision=lax.Precision.HIGHEST
    ).reshape(group_size, top_count)
    scores = jax.nn.sigmoid(router_logits[0])
    hot_float = expert_hot.reshape(group_size, top_count, expert_total).astype(jnp.float32)
    chosen = jnp.sum(hot_float * scores[:, None, :], axis=2)
    chosen_total = jnp.sum(chosen, axis=1, keepdims=True)
    gates = route_scale * chosen / chosen_total
    mixture = jnp.sum(picked_gate * gates, axis=1, keepdims=True)
    d_chosen = (route_scale * picked_gate - mixture) / chosen_total
    d_scores = jnp.sum(hot_float * d_chosen[:, :, None], axis=1)
    logit_grad = (d_scores * scores * (1.0 - scores)).astype(jnp.bfloat16)
    grouped_input = lax.all_to_all(router_input[0], "dp", split_axis=1, concat_axis=0, tiled=True)
    router_term = jnp.einsum(
        "ge,gc->ec", logit_grad, grouped_input, preferred_element_type=jnp.float32
    )
    grad_router = lax.psum_scatter(router_term, "expert", scatter_dimension=0, tiled=True)
    picked_rows = jnp.dot(
        slot_place.T,
        rows_back.reshape(expert_total * slot_depth, feature_share),
        preferred_element_type=jnp.float32,
    )
    mixed = jnp.sum(
        gates[:, :, None] * picked_rows.reshape(group_size, top_count, feature_share), axis=1
    )
    router_part = jnp.dot(logit_grad, router_weight, preferred_element_type=jnp.float32)
    grad_input = (mixed + router_part).astype(jnp.bfloat16)[None]
    return (grad_input, grad_router)


def solution(mesh):
    placed = (
        P("expert", None, "dp"),
        P("expert", None, None),
        P("expert", None, None),
        P("expert", "dp", None),
        P(None, "dp"),
        P("expert", "dp", None),
        P("expert", "dp", None),
        P("expert", None, "dp"),
        P("expert", None, None),
        P("expert", None, None),
    )
    return jax.shard_map(
        local,
        mesh=mesh,
        in_specs=placed,
        out_specs=(P("expert", None, "dp"), P("expert", "dp")),
        check_vma=False,
    )
```

profile of v0, /device:TPU:0, one launch (start us, length us, event | category | flops | bytes accessed | tf_op | source)
XLA Modules:
  0.0 147.4 jit_solution(7802566168627807311)
XLA Ops:
  7.2 0.8 reshape_squeeze.3
  8.4 1.2 convolution_convert_fusion
  9.7 0.8 reshape.186
  10.5 5.2 %all-to-all-start = ((bf16[32,3,960]{2,1,0:T(4,128)(2,1)}), bf16[32,3,960]{2,1,0:T(4,128)(2,1)S(1)}, u32[]{:S(2)}, u32[]{:S(2)}) async-start(bf16[32,3,960]{2,1,0:T(4,128)(2,1)} %reshape.186), calls=%async_computation | async-start | bytes 524288 | tf_op jit(solution)/shard_map/all_to_all | solution.py:75
  15.7 0.8 all_to_all.62
  16.5 0.6 copy.46
  17.1 5.5 %all-to-all-done = bf16[32,3,960]{2,1,0:T(4,128)(2,1)S(1)} async-done(((bf16[32,3,960]{2,1,0:T(4,128)(2,1)}), bf16[32,3,960]{2,1,0:T(4,128)(2,1)S(1)}, u32[]{:S(2)}, u32[]{:S(2)}) %all-to-all-start) | async-done | bytes 184352 | tf_op jit(solution)/shard_map/all_to_all | solution.py:75
  22.6 4.9 %all-to-all-start.3 = ((bf16[2,4,960]{2,0,1:T(2,128)(2,1)}), bf16[2,4,960]{2,0,1:T(2,128)(2,1)S(1)}, u32[]{:S(2)}, u32[]{:S(2)}) async-start(bf16[2,4,960]{2,0,1:T(2,128)(2,1)} %copy.46), calls=%async_computation.3 | async-start | bytes 32768 | tf_op jit(solution)/shard_map/all_to_all | solution.py:120
  27.6 5.1 %fusion.12 = f32[4,24,1024]{2,1,0:T(8,128)} fusion(bf16[4,1024,960]{1,2,0:T(8,128)(2,1)} %param.17, bf16[4,24,960]{2,0,1:T(4,128)(2,1)S(1)} %bitcast.79), kind=kOutput, calls=%fused_computation.24 | convolution fusion | flops 188743680 | bytes 8441856 | tf_op jit(solution)/shard_map/esd,efd->esf/dot_general | solution.py:82
  33.1 36.3 %all-reduce.4.cloned.1.call-done = f32[96,1024]{1,0:T(8,128)} async-done(((f32[96,1024]{1,0:T(8,128)}), f32[96,1024]{1,0:T(8,128)}) %all-reduce.4.cloned.1.call-update) | async-done | bytes 393232 | tf_op jit(solution)/shard_map/psum | solution.py:86
  69.4 1.2 multiply_convert_fusion
  70.7 1.1 multiply_reduce_fusion
  71.9 0.7 copy.42
  72.6 3.6 %all-to-all-start.2 = ((bf16[4,24,2]{0,2,1:T(2,128)(2,1)}), bf16[4,24,2]{0,2,1:T(2,128)(2,1)S(1)}, u32[]{:S(2)}, u32[]{:S(2)}) async-start(bf16[4,24,2]{0,2,1:T(2,128)(2,1)} %copy.42), calls=%async_computation.2 | async-start | bytes 24576 | tf_op jit(solution)/shard_map/all_to_all | solution.py:104
  76.3 5.4 %fusion.41 = f32[4,24,960]{2,1,0:T(8,128)S(1)} fusion(bf16[4,24,1024]{2,1,0:T(8,128)(2,1)S(1)} %bitcast.81, bf16[4,960,1024]{2,1,0:T(8,128)(2,1)} %param.15), kind=kOutput, calls=%fused_computation.74 | convolution fusion | flops 188743680 | bytes 8429568 | tf_op jit(solution)/shard_map/esf,edf->esd/dot_general | solution.py:95
  82.0 0.4 fusion.20
  82.8 0.9 fusion.32
  83.7 5.4 %fusion = bf16[4,24,960]{2,1,0:T(8,128)(2,1)S(1)} fusion(f32[4,24,960]{2,1,0:T(8,128)S(1)} %fusion.41, bf16[4,24,1024]{2,1,0:T(8,128)(2,1)S(1)} %bitcast.80, bf16[4,960,1024]{2,1,0:T(8,128)(2,1)} %param.16), kind=kOutput, calls=%fused_computation.1 | convolution fusion | flops 188928000 | bytes 8613888 | tf_op jit(solution)/shard_map/esf,edf->esd/dot_general | solution.py:98
  89.0 0.8 copy.40
  89.9 4.2 %all-to-all-start.1 = ((bf16[4,24,960]{2,0,1:T(4,128)(2,1)}), bf16[4,24,960]{2,0,1:T(4,128)(2,1)S(1)}, u32[]{:S(2)}, u32[]{:S(2)}) async-start(bf16[4,24,960]{2,0,1:T(4,128)(2,1)} %copy.40), calls=%async_computation.1 | async-start | bytes 393216 | tf_op jit(solution)/shard_map/all_to_all | solution.py:103
  94.0 0.6 dynamic-slice
  95.3 42.5 %all-reduce.6.cloned.1.call-done = f32[32,960]{1,0:T(8,128)} async-done(((f32[32,960]{1,0:T(8,128)}), f32[32,960]{1,0:T(8,128)}) %all-reduce.6.cloned.1.call-update) | async-done | bytes 122896
  137.8 1.4 constant_dynamic-slice_fusion
  139.8 0.7 fusion.3
  (43 shorter events, 2.3 us)
Async XLA Ops:
  7.2 132.6 %copy-start = (bf16[32,960]{1,0:T(8,128)(2,1)S(1)}, bf16[32,960]{1,0:T(8,128)(2,1)}, u32[]{:S(2)}) copy-start(bf16[32,960]{1,0:T(8,128)(2,1)} %param.14) | copy-start | bytes 184324
  7.2 25.7 %copy-start.3 = (s32[1,8,8]{2,1,0:T(8,128)S(1)}, s32[1,8,8]{2,1,0:T(8,128)}, u32[]{:S(2)}) copy-start(s32[1,8,8]{2,1,0:T(8,128)} %param.12) | copy-start | bytes 772
  7.2 25.6 %copy-start.4 = (f32[1,8,32]{2,1,0:T(8,128)S(1)}, f32[1,8,32]{2,1,0:T(8,128)}, u32[]{:S(2)}) copy-start(f32[1,8,32]{2,1,0:T(8,128)} %param.11) | copy-start | bytes 3076
  7.2 62.2 %copy-start.1 = (bf16[4,24,1024]{2,1,0:T(8,128)(2,1)S(1)}, bf16[4,24,1024]{2,1,0:T(8,128)(2,1)}, u32[]{:S(2)}) copy-start(bf16[4,24,1024]{2,1,0:T(8,128)(2,1)} %param.18) | copy-start | bytes 589828
  7.2 62.2 %copy-start.2 = (bf16[4,24,1024]{2,1,0:T(8,128)(2,1)S(1)}, bf16[4,24,1024]{2,1,0:T(8,128)(2,1)}, u32[]{:S(2)}) copy-start(bf16[4,24,1024]{2,1,0:T(8,128)(2,1)} %param.19) | copy-start | bytes 589828
  10.5 12.1 %all-to-all-start = ((bf16[32,3,960]{2,1,0:T(4,128)(2,1)}), bf16[32,3,960]{2,1,0:T(4,128)(2,1)S(1)}, u32[]{:S(2)}, u32[]{:S(2)}) async-start(bf16[32,3,960]{2,1,0:T(4,128)(2,1)} %reshape.186), calls=%async_computation | async-start | bytes 524288 | tf_op jit(solution)/shard_map/all_to_all | solution.py:75
  22.6 10.5 %all-to-all-start.3 = ((bf16[2,4,960]{2,0,1:T(2,128)(2,1)}), bf16[2,4,960]{2,0,1:T(2,128)(2,1)S(1)}, u32[]{:S(2)}, u32[]{:S(2)}) async-start(bf16[2,4,960]{2,0,1:T(2,128)(2,1)} %copy.46), calls=%async_computation.3 | async-start | bytes 32768 | tf_op jit(solution)/shard_map/all_to_all | solution.py:120
  27.5 42.0 %all-reduce.4.cloned.1.call-start = ((), (), s32[]{:S(2)}) async-start(), calls=%async_computation.4 | async-start | bytes 786432 | tf_op jit(solution)/shard_map/psum | solution.py:86
  72.6 9.0 %all-to-all-start.2 = ((bf16[4,24,2]{0,2,1:T(2,128)(2,1)}), bf16[4,24,2]{0,2,1:T(2,128)(2,1)S(1)}, u32[]{:S(2)}, u32[]{:S(2)}) async-start(bf16[4,24,2]{0,2,1:T(2,128)(2,1)} %copy.42), calls=%async_computation.2 | async-start | bytes 24576 | tf_op jit(solution)/shard_map/all_to_all | solution.py:104
  76.2 61.6 %all-reduce.6.cloned.1.call-start = ((), (), s32[]{:S(2)}) async-start(), calls=%async_computation.5 | async-start | bytes 262144
  76.2 17.8 %copy-start.5 = (u32[32]{0:T(128)S(1)}, u32[32]{0:T(128)}, u32[]{:S(2)}) copy-start(u32[32]{0:T(128)} %constant.42) | copy-start | bytes 388
  89.9 49.3 %all-to-all-start.1 = ((bf16[4,24,960]{2,0,1:T(4,128)(2,1)}), bf16[4,24,960]{2,0,1:T(4,128)(2,1)S(1)}, u32[]{:S(2)}, u32[]{:S(2)}) async-start(bf16[4,24,960]{2,0,1:T(4,128)(2,1)} %copy.40), calls=%async_computation.1 | async-start | bytes 393216 | tf_op jit(solution)/shard_map/all_to_all | solution.py:103
Sparse Core Ops, SparseCore 0:
  32.9 36.5 all-reduce.3
  83.8 53.9 all-reduce.5
where the time goes:
time: 148 us; the launch traced here: 147 us
  waiting for transfers between devices  84.4 us (57%)
  matrix products  19.4 us (13%)
  starting transfers between devices  17.8 us (12%)
  between operations  14.9 us (10%)
  local copies, waits for them, and re-layouts  7.53 us (5%)
  other arithmetic  3.35 us (2%)
    unnamed x3, waiting for transfers between devices  42.5 us
    psum x1, waiting for transfers between devices, local(): hidden_grad = lax.psum(partial_hidden.reshape(row_total, hidden_size), 'dp')  36.3 us
    all_to_all x1, waiting for transfers between devices, local(): lax.all_to_all(outgoing.reshape(expert_total, slot_depth, feature_share),...  5.47 us
    dot_general x1, matrix products, local(): jnp.einsum('esf,edf->esd', grad_up, up_weight, preferred_element_type=jnp...  5.39 us
    dot_general x1, matrix products, local(): jnp.einsum('esf,edf->esd', grad_gate, gate_weight, preferred_element_type...  5.39 us
    all_to_all x1, starting transfers between devices, local(): lax.all_to_all(outgoing.reshape(expert_total, slot_depth, feature_share),...  5.2 us
    dot_general x1, matrix products, local(): jnp.einsum('esd,efd->esf', incoming, down_weight, preferred_element_type=...  5.13 us
    all_to_all x1, starting transfers between devices, local(): lax.all_to_all(router_input[0], 'dp', split_axis=1, concat_axis=0, tiled=...  4.87 us
  transfers between devices with their start and end apart: 6, of which 3 were waited for; matrix products, arithmetic and copies ran while one was open for 13% of the time, Pallas kernels for 0%

commit v1 on v0

--- a/solution.py
+++ b/solution.py
@@ -4,6 +4,12 @@
 from jax.sharding import PartitionSpec as P
 
 route_scale = 2.5
+
+
+def gather_and_add(x, axis):
+    parts = lax.all_gather(x, axis, axis=0, tiled=False)
+    acc = parts.sum(axis=0)
+    return acc
 
 
 def split_pair(values):
@@ -83,7 +89,7 @@
         "esd,efd->esf", incoming, down_weight, preferred_element_type=jnp.float32
     )
     row_total = local_experts * slot_count
-    hidden_grad = lax.psum(partial_hidden.reshape(row_total, hidden_size), "dp")
+    hidden_grad = gather_and_add(partial_hidden.reshape(row_total, hidden_size), "dp")
     grad_gate, grad_up, gate_grad = activation_backward(
         hidden_grad,
         gate_saved.reshape(row_total, hidden_size),

time: 148 us -> 140 us (0.946)
  waiting for transfers between devices: 84.4 us -> 72 us
  blocking collectives: 0 us -> 11.9 us
  starting transfers between devices: 17.8 us -> 12.7 us
    psum x1 -> x0, waiting for transfers between devices: 36.3 us -> none  [local(): hidden_grad = lax.psum(partial_hidden.reshape(row_total, hidden_size), 'dp')]
    all_gather x0 -> x1, waiting for transfers between devices: none -> 25.2 us  [gather_and_add(): parts = lax.all_gather(x, axis, axis=0, tiled=False)]
    all_to_all x0 -> x1, blocking collectives: none -> 11.9 us  [local(): lax.all_to_all(outgoing.reshape(expert_total, slot_depth, feature_share),...]
    all_to_all x1 -> x0, waiting for transfers between devices: 5.47 us -> none  [local(): lax.all_to_all(outgoing.reshape(expert_total, slot_depth, feature_share),...]
    all_to_all x1, waiting for transfers between devices: 0.01 us -> 5.33 us  [local(): lax.all_to_all(router_input[0], 'dp', split_axis=1, concat_axis=0, tiled=...]
    all_to_all x1 -> x0, starting transfers between devices: 5.2 us -> none  [local(): lax.all_to_all(outgoing.reshape(expert_total, slot_depth, feature_share),...]
    reduce_sum x0 -> x1, other arithmetic: none -> 1.55 us  [gather_and_add(): acc = parts.sum(axis=0)]
  transfers between devices with their start and end apart: 6 -> 5, of which waited for: 3 -> 3; matrix products, arithmetic and copies ran while one was open for 13% -> 10% of each run, Pallas kernels for 0% -> 0%
where the time goes in v1:
time: 140 us
  waiting for transfers between devices  72 us (51%)
  matrix products  19.4 us (14%)
  between operations  14.9 us (11%)
  starting transfers between devices  12.7 us (9%)
  blocking collectives  11.9 us (8%)
  local copies, waits for them, and re-layouts  6.2 us (4%)
  other arithmetic  2.78 us (2%)
    unnamed x3, waiting for transfers between devices  41.4 us
    all_gather x1, waiting for transfers between devices, gather_and_add(): parts = lax.all_gather(x, axis, axis=0, tiled=False)  25.2 us
    all_to_all x1, blocking collectives, local(): lax.all_to_all(outgoing.reshape(expert_total, slot_depth, feature_share),...  11.9 us
    dot_general x1, matrix products, local(): jnp.einsum('esf,edf->esd', grad_gate, gate_weight, preferred_element_type...  5.39 us
    dot_general x1, matrix products, local(): jnp.einsum('esf,edf->esd', grad_up, up_weight, preferred_element_type=jnp...  5.39 us
    all_to_all x1, waiting for transfers between devices, local(): lax.all_to_all(router_input[0], 'dp', split_axis=1, concat_axis=0, tiled=...  5.33 us
    dot_general x1, matrix products, local(): jnp.einsum('esd,efd->esf', incoming, down_weight, preferred_element_type=...  5.12 us
    all_to_all x1, starting transfers between devices, local(): lax.all_to_all(router_input[0], 'dp', split_axis=1, concat_axis=0, tiled=...  4.87 us
  transfers between devices with their start and end apart: 5, of which 3 were waited for; matrix products, arithmetic and copies ran while one was open for 10% of the time, Pallas kernels for 0%

profile of v1, /device:TPU:0, one launch (start us, length us, event | category | flops | bytes accessed | tf_op | source)
XLA Modules:
  0.0 139.8 jit_solution(8428201138624496408)
XLA Ops:
  7.3 0.9 reshape_squeeze.3
  8.5 1.2 convolution_convert_fusion
  9.9 11.9 %all_to_all.70 = bf16[32,3,960]{2,1,0:T(4,128)(2,1)S(1)} all-to-all(bf16[32,3,960]{2,1,0:T(4,128)(2,1)S(1)} %reshape.181), channel_id=1, replica_groups=mesh['dp'=4,'expert'=8] {'expert'}, dimensions={0} | all-to-all | bytes 368640 | tf_op jit(solution)/shard_map/all_to_all | solution.py:81
  21.9 5.1 %fusion.19 = f32[4,24,1024]{2,1,0:T(8,128)} fusion(bf16[4,1024,960]{1,2,0:T(8,128)(2,1)} %param.17, bf16[4,24,960]{2,0,1:T(4,128)(2,1)S(1)} %bitcast.83), kind=kOutput, calls=%fused_computation.29 | convolution fusion | flops 188743680 | bytes 8441856 | tf_op jit(solution)/shard_map/esd,efd->esf/dot_general | solution.py:88
  27.2 0.6 copy.46
  27.8 4.9 %all-to-all-start.3 = ((bf16[2,4,960]{2,0,1:T(2,128)(2,1)}), bf16[2,4,960]{2,0,1:T(2,128)(2,1)S(1)}, u32[]{:S(2)}, u32[]{:S(2)}) async-start(bf16[2,4,960]{2,0,1:T(2,128)(2,1)} %copy.46), calls=%async_computation.3 | async-start | bytes 32768 | tf_op jit(solution)/shard_map/all_to_all | solution.py:126
  33.0 0.2 fusion.25
  33.2 5.3 %all-to-all-done.3 = bf16[2,4,960]{2,0,1:T(2,128)(2,1)S(1)} async-done(((bf16[2,4,960]{2,0,1:T(2,128)(2,1)}), bf16[2,4,960]{2,0,1:T(2,128)(2,1)S(1)}, u32[]{:S(2)}, u32[]{:S(2)}) %all-to-all-start.3) | async-done | bytes 15392 | tf_op jit(solution)/shard_map/all_to_all | solution.py:126
  38.5 25.2 %all-gather.2.cloned.1.call-done = f32[4,96,1024]{2,1,0:T(8,128)} async-done(((f32[1,96,1024]{2,1,0:T(8,128)}), f32[4,96,1024]{2,1,0:T(8,128)}) %all-gather.2.cloned.1.call-update) | async-done | bytes 1572880 | tf_op jit(solution)/shard_map/all_gather | solution.py:10
  63.7 1.6 %reduce_sum.81 = f32[96,1024]{1,0:T(8,128)S(1)} reduce(f32[4,96,1024]{2,1,0:T(8,128)} %all-gather.2.cloned.1.call-done, f32[]{:T(128)} %constant.24.clone.1), dimensions={0}, to_apply=%region_4.5 | reduce | flops 294912 | bytes 1966084 | tf_op jit(solution)/shard_map/reduce_sum | solution.py:11
  65.5 0.7 copy.42
  66.2 3.6 %all-to-all-start.2 = ((bf16[4,24,2]{0,2,1:T(2,128)(2,1)}), bf16[4,24,2]{0,2,1:T(2,128)(2,1)S(1)}, u32[]{:S(2)}, u32[]{:S(2)}) async-start(bf16[4,24,2]{0,2,1:T(2,128)(2,1)} %copy.42), calls=%async_computation.2 | async-start | bytes 24576 | tf_op jit(solution)/shard_map/all_to_all | solution.py:110
  69.9 5.4 %fusion.17 = f32[4,24,960]{2,1,0:T(8,128)S(1)} fusion(bf16[4,960,1024]{2,1,0:T(8,128)(2,1)} %param.15, bf16[4,24,1024]{2,1,0:T(8,128)(2,1)S(1)} %copy-done.1, f32[4,24,1024]{2,1,0:T(8,128)S(1)} %bitcast.78, bf16[4,24,1024]{2,1,0:T(8,128)(2,1)S(1)} %copy-done.2), kind=kOutput, calls=%fused_computation.28 | convolution fusion | flops 189923328 | bytes 9019392 | tf_op jit(solution)/shard_map/esf,edf->esd/dot_general | solution.py:101
  75.6 0.4 fusion.30
  76.0 0.2 multiply_reduce_fusion.2
  76.4 0.9 fusion.42
  77.3 5.4 %fusion = bf16[4,24,960]{2,1,0:T(8,128)(2,1)S(1)} fusion(f32[4,24,960]{2,1,0:T(8,128)S(1)} %fusion.17, bf16[4,960,1024]{2,1,0:T(8,128)(2,1)} %param.16, f32[4,24,1024]{2,1,0:T(8,128)S(1)} %bitcast.79, bf16[4,24,1024]{2,1,0:T(8,128)(2,1)S(1)} %copy-done.1), kind=kOutput, calls=%fused_computation.1 | convolution fusion | flops 189616128 | bytes 9007104 | tf_op jit(solution)/shard_map/esf,edf->esd/dot_general | solution.py:104
  82.6 0.8 copy.40
  83.5 4.2 %all-to-all-start.1 = ((bf16[4,24,960]{2,0,1:T(4,128)(2,1)}), bf16[4,24,960]{2,0,1:T(4,128)(2,1)S(1)}, u32[]{:S(2)}, u32[]{:S(2)}) async-start(bf16[4,24,960]{2,0,1:T(4,128)(2,1)} %copy.40), calls=%async_computation.1 | async-start | bytes 393216 | tf_op jit(solution)/shard_map/all_to_all | solution.py:109
  87.6 0.6 dynamic-slice
  88.9 41.4 %all-reduce.3.cloned.1.call-done = f32[32,960]{1,0:T(8,128)} async-done(((f32[32,960]{1,0:T(8,128)}), f32[32,960]{1,0:T(8,128)}) %all-reduce.3.cloned.1.call-update) | async-done | bytes 122896
  130.3 1.4 constant_dynamic-slice_fusion
  132.0 0.3 fusion.1
  132.2 0.7 fusion.3
  (45 shorter events, 2.1 us)
Async XLA Ops:
  7.2 125.1 %copy-start = (bf16[32,960]{1,0:T(8,128)(2,1)S(1)}, bf16[32,960]{1,0:T(8,128)(2,1)}, u32[]{:S(2)}) copy-start(bf16[32,960]{1,0:T(8,128)(2,1)} %param.14) | copy-start | bytes 184324
  7.2 25.6 %copy-start.3 = (s32[1,8,8]{2,1,0:T(8,128)S(1)}, s32[1,8,8]{2,1,0:T(8,128)}, u32[]{:S(2)}) copy-start(s32[1,8,8]{2,1,0:T(8,128)} %param.12) | copy-start | bytes 772
  7.2 19.9 %copy-start.5 = (bf16[1,2,3840]{2,1,0:T(2,128)(2,1)S(1)}, bf16[1,2,3840]{2,1,0:T(2,128)(2,1)}, u32[]{:S(2)}) copy-start(bf16[1,2,3840]{2,1,0:T(2,128)(2,1)} %param.13) | copy-start | bytes 46084
  7.2 25.6 %copy-start.4 = (f32[1,8,32]{2,1,0:T(8,128)S(1)}, f32[1,8,32]{2,1,0:T(8,128)}, u32[]{:S(2)}) copy-start(f32[1,8,32]{2,1,0:T(8,128)} %param.11) | copy-start | bytes 3076
  7.2 25.6 %copy-start.1 = (bf16[4,24,1024]{2,1,0:T(8,128)(2,1)S(1)}, bf16[4,24,1024]{2,1,0:T(8,128)(2,1)}, u32[]{:S(2)}) copy-start(bf16[4,24,1024]{2,1,0:T(8,128)(2,1)} %param.18) | copy-start | bytes 589828
  7.2 25.6 %copy-start.2 = (bf16[4,24,1024]{2,1,0:T(8,128)(2,1)S(1)}, bf16[4,24,1024]{2,1,0:T(8,128)(2,1)}, u32[]{:S(2)}) copy-start(bf16[4,24,1024]{2,1,0:T(8,128)(2,1)} %param.19) | copy-start | bytes 589828
  7.2 56.5 %all-gather.2.cloned.1.call-start = ((), (), s32[]{:S(2)}) async-start(), calls=%async_computation.4 | async-start | bytes 1966080 | tf_op jit(solution)/shard_map/all_gather | solution.py:10
  27.8 10.7 %all-to-all-start.3 = ((bf16[2,4,960]{2,0,1:T(2,128)(2,1)}), bf16[2,4,960]{2,0,1:T(2,128)(2,1)S(1)}, u32[]{:S(2)}, u32[]{:S(2)}) async-start(bf16[2,4,960]{2,0,1:T(2,128)(2,1)} %copy.46), calls=%async_computation.3 | async-start | bytes 32768 | tf_op jit(solution)/shard_map/all_to_all | solution.py:126
  66.2 9.0 %all-to-all-start.2 = ((bf16[4,24,2]{0,2,1:T(2,128)(2,1)}), bf16[4,24,2]{0,2,1:T(2,128)(2,1)S(1)}, u32[]{:S(2)}, u32[]{:S(2)}) async-start(bf16[4,24,2]{0,2,1:T(2,128)(2,1)} %copy.42), calls=%async_computation.2 | async-start | bytes 24576 | tf_op jit(solution)/shard_map/all_to_all | solution.py:110
  69.8 60.5 %all-reduce.3.cloned.1.call-start = ((), (), s32[]{:S(2)}) async-start(), calls=%async_computation.5 | async-start | bytes 262144
  69.8 17.8 %copy-start.6 = (u32[32]{0:T(128)S(1)}, u32[32]{0:T(128)}, u32[]{:S(2)}) copy-start(u32[32]{0:T(128)} %constant.42) | copy-start | bytes 388
  83.5 48.2 %all-to-all-start.1 = ((bf16[4,24,960]{2,0,1:T(4,128)(2,1)}), bf16[4,24,960]{2,0,1:T(4,128)(2,1)S(1)}, u32[]{:S(2)}, u32[]{:S(2)}) async-start(bf16[4,24,960]{2,0,1:T(4,128)(2,1)} %copy.40), calls=%async_computation.1 | async-start | bytes 393216 | tf_op jit(solution)/shard_map/all_to_all | solution.py:109
Sparse Core Ops, SparseCore 0:
  27.2 36.4 all-gather.1
  77.4 52.8 all-reduce.2
